TPU v7x, 256 devices: a whole 4x4x8 slice. The times are simulated.
256 devices in a mesh: dp: 8 (over z_hi, core), comp: 32 (over x, z_lo, y).
Axes of the slice: x: 4, y: 4, z: 8 (z_hi: 4, z_lo: 2; z = z_hi * 2 + z_lo), core: 2. Of those that a mesh axis runs over, the one named last changes fastest.
Arguments:
- row_ids: int32 [8192], P('dp'), may hold values from 0 to 8191
- table: float32 [8192, 1024], P('comp'), may hold values from -25 to 25, as said below
- means: float32 [16384, 1024], P('comp'), may hold values from -0.3 to 0.3
- precisions: float32 [16384, 1024], P('comp'), may hold values from 0.8 to 1.2
- mix_logits: float32 [16384], P('comp'), may hold values from -2 to 2
- step_index: int32 [1], replicated, may hold values from 0 to 65535
Outputs:
- new_means: float32 [16384, 1024], P('comp')
- new_precisions: float32 [16384, 1024], P('comp')
- new_logits: float32 [16384], P('comp')
Inputs may be any that keep to these rules, and one draw needn't show every extreme that they name: `table`: embedding rows with entries of order one and row scales that differ.
All inputs are finite; a program needn't handle non-finite values.
Results may differ from a plain program's by a relative error of at most 0.0014.
Values sent between devices are 32-bit elements; how exact they have to be, the bound alone decides.
A program may use at most 64 MiB of HBM per device.

v0:
```python
import jax
import jax.numpy as jnp
from jax import lax
from jax.sharding import PartitionSpec as P


def split(value):
    high = lax.reduce_precision(value, 8, 7)
    return (high.astype(jnp.bfloat16), (value - high).astype(jnp.bfloat16))


def product(left, right, dims):

    def one(a, b):
        return lax.dot_general(a, b, (dims, ((), ())), preferred_element_type=jnp.float32)

    return one(left[0], right[0]) + (one(left[0], right[1]) + one(left[1], right[0]))


def multiplicity(ids, part, parts, owners, share):
    per_owner = parts * share
    owner = ids // per_owner
    within = ids % per_owner
    mine = within // share == part
    row = within % share
    left = (owner[None, :] == lax.broadcasted_iota(jnp.int32, (owners, 1), 0)) & mine[None, :]
    right = row[None, :] == lax.broadcasted_iota(jnp.int32, (share, 1), 0)
    found = lax.dot_general(
        left.astype(jnp.bfloat16),
        right.astype(jnp.bfloat16),
        (((1,), (1,)), ((), ())),
        preferred_element_type=jnp.float32,
    )
    return found.reshape(-1)


def local(row_ids, table, means, precisions, mix_logits, step_index):
    dp, comp = (lax.axis_size("dp"), lax.axis_size("comp"))
    part = lax.axis_index("dp")
    share = table.shape[0] // dp
    batch = 1.0 * row_ids.shape[0] * dp
    ids = lax.all_gather(row_ids, "dp", tiled=True)
    mine = lax.dynamic_slice_in_dim(table, part * share, share, 0)
    samples = lax.all_gather(mine, "comp", tiled=True)
    times = multiplicity(ids, part, dp, comp, share)
    squares = samples * samples
    s, q = (split(samples), split(squares))
    excess = precisions - 1.0
    cross = -2.0 * precisions * means
    e, c = (split(excess), split(cross))
    offset = (
        mix_logits
        + 0.5 * jnp.sum(jnp.log(precisions), axis=1)
        - 0.5 * jnp.sum(precisions * means * means, axis=1)
    )
    lanes = ((1,), (1,))
    quadratic = product(e, q, lanes) + product(c, s, lanes)
    scores = offset[:, None] - 0.5 * quadratic
    top = jnp.max(scores, axis=0)
    raised = jnp.exp(scores - top[None, :])
    mass = jnp.sum(raised, axis=0)
    logit_top = jnp.max(mix_logits)
    logit_raised = jnp.exp(mix_logits - logit_top)
    logit_mass = jnp.sum(logit_raised)
    packed = jnp.concatenate([top, mass, jnp.full((128,), logit_top), jnp.full((128,), logit_mass)])
    every = lax.all_gather(packed, "comp")
    rows = top.shape[0]
    tops, masses = (every[:, :rows], every[:, rows : 2 * rows])
    peak = jnp.max(tops, axis=0)
    total = jnp.sum(masses * jnp.exp(tops - peak[None, :]), axis=0)
    factor = jnp.exp(top - peak) / total * times
    resp = raised * factor[None, :]
    logit_tops, logit_masses = (every[:, 2 * rows], every[:, 2 * rows + 128])
    logit_peak = jnp.max(logit_tops)
    logit_total = jnp.sum(logit_masses * jnp.exp(logit_tops - logit_peak))
    weights = logit_raised * (jnp.exp(logit_top - logit_peak) / logit_total)
    counts = jnp.sum(resp, axis=1)
    r = split(resp)
    inner = ((1,), (0,))
    first = product(r, s, inner)
    second = product(r, q, inner)
    first, second = (
        lax.psum_scatter(x, "dp", scatter_dimension=0, tiled=True) for x in (first, second)
    )
    counts = lax.psum(counts, "dp")

    def own(x):
        size = x.shape[0] // dp
        return lax.dynamic_slice_in_dim(x, part * size, size, 0)

    step = (2.0 + step_index[0].astype(jnp.float32) / 8192.0) ** (-0.6)
    retain = 1.0 - step
    mass_all = retain * weights + step * counts / batch
    new_logits = jnp.log(mass_all)
    mass_new = own(mass_all)[:, None]
    prior = own(retain * weights)[:, None]
    own_counts = own(counts)[:, None]
    own_means = own(means)
    new_means = (prior * own_means + step * first / batch) / mass_new
    moved = own_means - new_means
    spread = (
        prior * (1.0 / own(precisions) + moved * moved)
        + step * (second - 2.0 * new_means * first + new_means * new_means * own_counts) / batch
    )
    new_precisions = mass_new / spread
    new_means, new_precisions = (
        lax.all_gather(x, "dp", tiled=True) for x in (new_means, new_precisions)
    )
    return (new_means, new_precisions, new_logits)


def solution(mesh):
    placed = (P("dp"), P("comp", None), P("comp", None), P("comp", None), P("comp"), P())
    return jax.shard_map(
        local,
        mesh=mesh,
        in_specs=placed,
        out_specs=(P("comp", None), P("comp", None), P("comp")),
        check_vma=False,
    )
```

profile of v0, /device:TPU:1, one launch (start us, length us, event | category | flops | bytes accessed | tf_op | source)
XLA Modules:
  0.0 447.8 jit_solution(17200917461490478965)
XLA Ops:
  9.1 19.7 %all_gather.21 = s32[8192]{0:T(1024)S(1)} all-gather(s32[1024]{0:T(1024)} %param.6), channel_id=1, replica_groups=mesh['dp'=8,'comp'=32] {'dp'}, dimensions={0}, use_global_device_ids=true | all-gather | bytes 36864 | tf_op jit(solution)/shard_map/all_gather | solution.py:42
  30.7 3.8 log_reduce_fusion
  35.7 118.0 %all-gather.6.cloned.1.call-done = f32[1024,1024]{1,0:T(8,128)} async-done(((f32[32,1024]{1,0:T(8,128)}), f32[1024,1024]{1,0:T(8,128)}) %all-gather.6.cloned.1.call-update) | async-done | bytes 4194320 | tf_op jit(solution)/shard_map/all_gather | solution.py:44
  153.7 2.9 reduce-precision_convert_fusion.1
  156.6 1.3 fusion.10
  158.0 1.3 fusion.27
  159.3 1.3 fusion.44
  161.5 1.3 fusion.18
  162.8 1.4 fusion.25
  165.0 1.7 fusion.43
  168.3 68.0 %all-gather.1 = f32[32,1,2304]{2,1,0:T(1,128)S(1)} all-gather(f32[1,1,2304]{2,1,0:T(1,128)S(1)} %reshape.45), channel_id=2, replica_groups=mesh['dp'=8,'comp'=32] {'comp'}, dimensions={0}, use_global_device_ids=true | all-gather | bytes 304128 | tf_op jit(solution)/shard_map/all_gather | solution.py:66
  238.1 1.3 fusion.16
  239.4 2.6 add_add_fusion.1
  242.2 3.3 fusion.46
  245.6 1.3 fusion.23
  247.2 2.6 add_add_fusion
  254.4 48.7 %psum.7 = f32[512]{0:T(512)S(1)} all-reduce(f32[512]{0:T(512)S(1)} %get-tuple-element.13), channel_id=1, replica_groups=mesh['dp'=8,'comp'=32] {'dp'}, use_global_device_ids=true, to_apply=%region_12.13 | all-reduce | flops 512 | bytes 4096 | tf_op jit(solution)/shard_map/psum | solution.py:85
  304.4 10.1 %reduce-scatter.3.cloned.1.call-done = f32[64,1024]{1,0:T(8,128)} async-done(((f32[512,1024]{1,0:T(8,128)}), f32[64,1024]{1,0:T(8,128)}) %reduce-scatter.3.cloned.1.call-update) | async-done | bytes 262160 | tf_op jit(solution)/shard_map/reduce_scatter | solution.py:83
  314.5 46.2 %reduce-scatter.5.cloned.1.call-done = f32[64,1024]{1,0:T(8,128)} async-done(((f32[512,1024]{1,0:T(8,128)}), f32[64,1024]{1,0:T(8,128)}) %reduce-scatter.5.cloned.1.call-update) | async-done | bytes 262160 | tf_op jit(solution)/shard_map/reduce_scatter | solution.py:83
  360.7 2.2 add_divide_fusion
  363.5 36.6 %all-gather.8.cloned.1.call-done = f32[512,1024]{1,0:T(8,128)} async-done(((f32[64,1024]{1,0:T(8,128)}), f32[512,1024]{1,0:T(8,128)}) %all-gather.8.cloned.1.call-update) | async-done | bytes 2097168 | tf_op jit(solution)/shard_map/all_gather | solution.py:107
  400.2 36.4 %all-gather.10.cloned.1.call-done = f32[512,1024]{1,0:T(8,128)} async-done(((f32[64,1024]{1,0:T(8,128)}), f32[512,1024]{1,0:T(8,128)}) %all-gather.10.cloned.1.call-update) | async-done | bytes 2097168 | tf_op jit(solution)/shard_map/all_gather | solution.py:107
  436.6 3.3 copy.15
  439.9 1.3 copy.16
  (60 shorter events, 14.4 us)
Async XLA Ops:
  7.2 1.2 copy-start
  7.2 146.5 %all-gather.6.cloned.1.call-start = ((), (), s32[]{:S(2)}) async-start(), calls=%async_computation.2 | async-start | bytes 4325376 | tf_op jit(solution)/shard_map/all_gather | solution.py:44
  9.1 305.4 %reduce-scatter.3.cloned.1.call-start = ((), (), s32[]{:S(2)}) async-start(), calls=%async_computation.3 | async-start | bytes 2359296 | tf_op jit(solution)/shard_map/reduce_scatter | solution.py:83
  30.7 3.8 copy-start.12
  35.7 120.9 %copy-start.1 = (f32[512,1024]{1,0:T(8,128)S(1)}, f32[512,1024]{1,0:T(8,128)}, u32[]{:S(2)}) copy-start(f32[512,1024]{1,0:T(8,128)} %param.9) | copy-start | bytes 6291460
  156.6 1.3 copy-start.7
  157.9 1.3 copy-start.11
  159.3 2.2 copy-start.4
  162.8 1.6 copy-start.2
  162.8 2.2 copy-start.3
  236.9 1.3 copy-start.9
  242.1 118.6 %reduce-scatter.5.cloned.1.call-start = ((), (), s32[]{:S(2)}) async-start(), calls=%async_computation.5 | async-start | bytes 2359296 | tf_op jit(solution)/shard_map/reduce_scatter | solution.py:83
  242.1 3.3 copy-start.5
  242.1 3.4 copy-start.10
  245.6 1.6 copy-start.8
  249.8 150.4 %all-gather.8.cloned.1.call-start = ((), (), s32[]{:S(2)}) async-start(), calls=%async_computation.4 | async-start | bytes 2359296 | tf_op jit(solution)/shard_map/all_gather | solution.py:107
  362.9 73.6 %all-gather.10.cloned.1.call-start = ((), (), s32[]{:S(2)}) async-start(), calls=%async_computation.6 | async-start | bytes 2359296 | tf_op jit(solution)/shard_map/all_gather | solution.py:107
  436.6 3.3 copy-start.6
Sparse Core Ops, SparseCore 0:
  10.4 143.2 all-gather.5
  242.2 72.2 reduce-scatter.2
  317.6 43.0 reduce-scatter.4
  363.1 37.0 all-gather.7
  402.5 34.0 all-gather.9
where the time goes:
time: 448 us
  waiting for transfers between devices  248 us (55%)
  blocking collectives  136 us (30%)
  matrix products  21.1 us (5%)
  between operations  16.7 us (4%)
  other arithmetic  15.3 us (3%)
  local copies, waits for them, and re-layouts  10.1 us (2%)
    all_gather x1, waiting for transfers between devices, local(): samples = lax.all_gather(mine, 'comp', tiled=True)  118 us
    all_gather x2, waiting for transfers between devices, local(): lax.all_gather(x, 'dp', tiled=True)  73.1 us
    all_gather x1, blocking collectives, local(): every = lax.all_gather(packed, 'comp')  68 us
    reduce_scatter x2, waiting for transfers between devices, local(): lax.psum_scatter(x, 'dp', scatter_dimension=0, tiled=True)  56.3 us
    psum x1, blocking collectives, local(): counts = lax.psum(counts, 'dp')  48.7 us
    dot_general x12, matrix products, one(): lax.dot_general(a, b, (dims, ((), ())), preferred_element_type=jnp.float32)  20.6 us
    all_gather x1, blocking collectives, local(): ids = lax.all_gather(row_ids, 'dp', tiled=True)  19.7 us
  transfers between devices with their start and end apart: 5, of which 5 were waited for; matrix products, arithmetic and copies ran while one was open for 4% of the time, Pallas kernels for 0%

commit v1 on v0

--- a/solution.py
+++ b/solution.py
@@ -41,7 +41,12 @@
     batch = 1.0 * row_ids.shape[0] * dp
     ids = lax.all_gather(row_ids, "dp", tiled=True)
     mine = lax.dynamic_slice_in_dim(table, part * share, share, 0)
-    samples = lax.all_gather(mine, "comp", tiled=True)
+    buffers = []
+    for _ in range(jax.lax.axis_size("comp")):
+        buffers.append(mine)
+    everything = jnp.stack(buffers)
+    low = jax.lax.all_to_all(everything, "comp", 0, 0)
+    samples = jnp.concatenate(low, axis=0)
     times = multiplicity(ids, part, dp, comp, share)
     squares = samples * samples
     s, q = (split(samples), split(squares))

time: 448 us -> 363 us (0.81)
  waiting for transfers between devices: 248 us -> 129 us
  blocking collectives: 136 us -> 160 us
  starting transfers between devices: 0.21 us -> 9.65 us
    all_gather x1 -> x0, waiting for transfers between devices: 118 us -> none  [local(): samples = lax.all_gather(mine, 'comp', tiled=True)]
    all_gather x1, blocking collectives: 19.7 us -> 65.8 us  [local(): ids = lax.all_gather(row_ids, 'dp', tiled=True)]
    psum x1, blocking collectives: 48.7 us -> 28.2 us  [local(): counts = lax.psum(counts, 'dp')]
    all_to_all x0 -> x1, starting transfers between devices: none -> 9.48 us  [local(): low = jax.lax.all_to_all(everything, 'comp', 0, 0)]
  transfers between devices with their start and end apart: 5 -> 5, of which waited for: 5 -> 4; matrix products, arithmetic and copies ran while one was open for 4% -> 4% of each run, Pallas kernels for 0% -> 0%
where the time goes in v1:
time: 363 us
  blocking collectives  160 us (44%)
  waiting for transfers between devices  129 us (36%)
  matrix products  21.1 us (6%)
  between operations  16.7 us (5%)
  other arithmetic  15.4 us (4%)
  local copies, waits for them, and re-layouts  10.9 us (3%)
  starting transfers between devices  9.65 us (3%)
    all_gather x2, waiting for transfers between devices, local(): lax.all_gather(x, 'dp', tiled=True)  73.5 us
    all_gather x1, blocking collectives, local(): every = lax.all_gather(packed, 'comp')  66.5 us
    all_gather x1, blocking collectives, local(): ids = lax.all_gather(row_ids, 'dp', tiled=True)  65.8 us
    reduce_scatter x2, waiting for transfers between devices, local(): lax.psum_scatter(x, 'dp', scatter_dimension=0, tiled=True)  54.7 us
    psum x1, blocking collectives, local(): counts = lax.psum(counts, 'dp')  28.2 us
    dot_general x12, matrix products, one(): lax.dot_general(a, b, (dims, ((), ())), preferred_element_type=jnp.float32)  20.6 us
    all_to_all x1, starting transfers between devices, local(): low = jax.lax.all_to_all(everything, 'comp', 0, 0)  9.48 us
  transfers between devices with their start and end apart: 5, of which 4 were waited for; matrix products, arithmetic and copies ran while one was open for 4% of the time, Pallas kernels for 0%

profile of v1, /device:TPU:1, one launch (start us, length us, event | category | flops | bytes accessed | tf_op | source)
XLA Modules:
  0.0 362.9 jit_solution(6510420617838256857)
XLA Ops:
  8.4 2.5 stack.2
  10.9 9.5 %all-to-all-start = ((f32[32,32,1024]{2,1,0:T(8,128)}), f32[32,32,1024]{2,1,0:T(8,128)}, u32[]{:S(2)}, u32[]{:S(2)}) async-start(f32[32,32,1024]{2,1,0:T(8,128)} %stack.2), calls=%async_computation | async-start | bytes 8388608 | tf_op jit(solution)/shard_map/all_to_all | solution.py:48
  20.5 65.8 %all_gather.17 = s32[8192]{0:T(1024)S(1)} all-gather(s32[1024]{0:T(1024)S(1)} %copy-done.12), channel_id=1, replica_groups=mesh['dp'=8,'comp'=32] {'dp'}, dimensions={0}, use_global_device_ids=true | all-gather | bytes 36864 | tf_op jit(solution)/shard_map/all_gather | solution.py:42
  87.5 3.3 log_reduce_fusion
  92.1 3.9 %fusion = (bf16[1024,1024]{1,0:T(8,128)(2,1)S(1)}, bf16[1024,1024]{1,0:T(8,128)(2,1)S(1)}, bf16[1024,1024]{1,0:T(8,128)(2,1)S(1)}, bf16[1024,1024]{1,0:T(8,128)(2,1)S(1)}) fusion(f32[32,32,1024]{2,1,0:T(8,128)} %all-to-all-done), kind=kLoop, calls=%fused_computation.4 | loop fusion | flops 9437184 | bytes 12582912 | tf_op jit(solution)/shard_map/convert_element_type | solution.py:9
  96.0 1.3 fusion.10
  97.3 1.3 fusion.20
  98.6 1.3 fusion.37
  99.9 1.3 fusion.38
  101.2 1.3 fusion.19
  103.5 1.8 fusion.36
  106.9 66.5 %all-gather.1 = f32[32,1,2304]{2,1,0:T(1,128)S(1)} all-gather(f32[1,1,2304]{2,1,0:T(1,128)S(1)} %reshape.51), channel_id=2, replica_groups=mesh['dp'=8,'comp'=32] {'comp'}, dimensions={0}, use_global_device_ids=true | all-gather | bytes 304128 | tf_op jit(solution)/shard_map/all_gather | solution.py:71
  176.5 2.7 add_add_fusion.1
  179.3 3.3 fusion.42
  182.6 1.3 fusion.41
  183.9 2.6 add_add_fusion
  191.2 28.2 %psum.7 = f32[512]{0:T(512)S(1)} all-reduce(f32[512]{0:T(512)S(1)} %get-tuple-element.15), channel_id=1, replica_groups=mesh['dp'=8,'comp'=32] {'dp'}, use_global_device_ids=true, to_apply=%region_12.13 | all-reduce | flops 512 | bytes 4096 | tf_op jit(solution)/shard_map/psum | solution.py:90
  220.8 8.3 %reduce-scatter.3.cloned.1.call-done = f32[64,1024]{1,0:T(8,128)} async-done(((f32[512,1024]{1,0:T(8,128)}), f32[64,1024]{1,0:T(8,128)}) %reduce-scatter.3.cloned.1.call-update) | async-done | bytes 262160 | tf_op jit(solution)/shard_map/reduce_scatter | solution.py:88
  229.1 46.3 %reduce-scatter.5.cloned.1.call-done = f32[64,1024]{1,0:T(8,128)} async-done(((f32[512,1024]{1,0:T(8,128)}), f32[64,1024]{1,0:T(8,128)}) %reduce-scatter.5.cloned.1.call-update) | async-done | bytes 262160 | tf_op jit(solution)/shard_map/reduce_scatter | solution.py:88
  275.4 2.2 add_divide_fusion
  278.3 37.1 %all-gather.5.cloned.1.call-done = f32[512,1024]{1,0:T(8,128)} async-done(((f32[64,1024]{1,0:T(8,128)}), f32[512,1024]{1,0:T(8,128)}) %all-gather.5.cloned.1.call-update) | async-done | bytes 2097168 | tf_op jit(solution)/shard_map/all_gather | solution.py:112
  315.4 36.4 %all-gather.7.cloned.1.call-done = f32[512,1024]{1,0:T(8,128)} async-done(((f32[64,1024]{1,0:T(8,128)}), f32[512,1024]{1,0:T(8,128)}) %all-gather.7.cloned.1.call-update) | async-done | bytes 2097168 | tf_op jit(solution)/shard_map/all_gather | solution.py:112
  351.8 3.3 copy.15
  355.1 1.3 copy.16
  (60 shorter events, 13.4 us)
Async XLA Ops:
  7.2 1.2 copy-start
  10.9 9.5 %copy-start.12 = (s32[1024]{0:T(1024)S(1)}, s32[1024]{0:T(1024)}, u32[]{:S(2)}) copy-start(s32[1024]{0:T(1024)} %param.6) | copy-start | bytes 12292
  10.9 76.0 %copy-start.11 = (f32[512]{0:T(512)S(1)}, f32[512]{0:T(512)}, u32[]{:S(2)}) copy-start(f32[512]{0:T(512)} %param.10) | copy-start | bytes 6148
  10.9 76.6 %copy-start.1 = (f32[512,1024]{1,0:T(8,128)S(1)}, f32[512,1024]{1,0:T(8,128)}, u32[]{:S(2)}) copy-start(f32[512,1024]{1,0:T(8,128)} %param.9) | copy-start | bytes 6291460
  10.9 81.1 %all-to-all-start = ((f32[32,32,1024]{2,1,0:T(8,128)}), f32[32,32,1024]{2,1,0:T(8,128)}, u32[]{:S(2)}, u32[]{:S(2)}) async-start(f32[32,32,1024]{2,1,0:T(8,128)} %stack.2), calls=%async_computation | async-start | bytes 8388608 | tf_op jit(solution)/shard_map/all_to_all | solution.py:48
  20.4 208.7 %reduce-scatter.3.cloned.1.call-start = ((), (), s32[]{:S(2)}) async-start(), calls=%async_computation.3 | async-start | bytes 2359296 | tf_op jit(solution)/shard_map/reduce_scatter | solution.py:88
  96.0 1.3 copy-start.5
  96.0 5.2 %copy-start.7 = (bf16[1024,1024]{1,0:T(8,128)(2,1)}, bf16[1024,1024]{1,0:T(8,128)(2,1)S(1)}, u32[]{:S(2)}) copy-start(bf16[1024,1024]{1,0:T(8,128)(2,1)S(1)} %get-tuple-element.9) | copy-start | bytes 6291460
  97.3 1.3 copy-start.10
  101.2 1.6 copy-start.2
  101.2 2.2 copy-start.3
  174.0 1.3 copy-start.8
  179.2 96.2 %reduce-scatter.5.cloned.1.call-start = ((), (), s32[]{:S(2)}) async-start(), calls=%async_computation.5 | async-start | bytes 2359296 | tf_op jit(solution)/shard_map/reduce_scatter | solution.py:88
  179.2 3.3 copy-start.6
  179.3 3.3 copy-start.9
  186.5 128.8 %all-gather.5.cloned.1.call-start = ((), (), s32[]{:S(2)}) async-start(), calls=%async_computation.4 | async-start | bytes 2359296 | tf_op jit(solution)/shard_map/all_gather | solution.py:112
  277.7 74.1 %all-gather.7.cloned.1.call-start = ((), (), s32[]{:S(2)}) async-start(), calls=%async_computation.6 | async-start | bytes 2359296 | tf_op jit(solution)/shard_map/all_gather | solution.py:112
  351.8 3.3 copy-start.4
Sparse Core Ops, SparseCore 0:
  179.3 49.7 reduce-scatter.2
  232.2 43.1 reduce-scatter.4
  277.9 37.4 all-gather.4
  317.6 34.0 all-gather.6
